TPU v7x, 256 devices: a whole 4x4x8 slice. The times are simulated.
256 devices in a mesh: row: 8 (over y, z_lo), col: 4 (over x), band: 8 (over z_hi, core).
Axes of the slice: x: 4, y: 4, z: 8 (z_hi: 4, z_lo: 2; z = z_hi * 2 + z_lo), core: 2. Of those that a mesh axis runs over, the one named last changes fastest.
Arguments:
- noisy: float32 [224, 128, 4096], P('band', 'row', 'col'), may hold values from -4 to 4
- weight_map: float32 [128, 4096], P('row', 'col'), may hold values from 1.5 to 12
Outputs:
- denoised: float32 [224, 128, 4096], P('band', 'row', 'col')
All inputs are finite; a program needn't handle non-finite values.
Results may differ from a plain program's by a relative error of at most 0.0001.
Values sent between devices are 32-bit elements; how exact they have to be, the bound alone decides.
A program may use at most 64 MiB of HBM per device.

v0:
```python
import jax
import jax.numpy as jnp
from jax import lax
from jax.sharding import PartitionSpec as P

ITERS = 4


dual_step = 0.35
primal_step = 0.35


def over_pieces(shard, axis):
    blocks = lax.all_gather(shard, axis)
    return blocks.sum(axis=0)


def with_halo(cells, sides, width):
    for axis, dim in sides:
        count = lax.axis_size(axis)
        ends = count - 1
        head = lax.slice_in_dim(cells, 0, width, axis=dim)
        tail = lax.slice_in_dim(cells, cells.shape[dim] - width, cells.shape[dim], axis=dim)
        cells = jnp.concatenate(
            [
                lax.ppermute(tail, axis, [(i, (i + 1) % count) for i in range(ends)]),
                cells,
                lax.ppermute(head, axis, [((i + 1) % count, i) for i in range(ends)]),
            ],
            axis=dim,
        )
    return cells


def pixel_scale(local_sum, weight):
    squares = over_pieces(local_sum, "band")
    return weight / jnp.maximum(weight, jnp.sqrt(1.0 + squares))


def local(noisy, weight_map):
    bands, rows, cols = noisy.shape
    total_rows = rows * lax.axis_size("row")
    total_cols = cols * lax.axis_size("col")
    margin = ITERS
    joined = jnp.concatenate([noisy, weight_map[None]], axis=0)
    framed = with_halo(joined, (("row", 1), ("col", 2)), margin)
    source = framed[:-1]
    weight = framed[-1]
    ext_rows = rows + 2 * margin
    ext_cols = cols + 2 * margin
    global_row = (
        lax.axis_index("row") * rows - margin + lax.broadcasted_iota(jnp.int32, (1, ext_rows, 1), 1)
    )
    global_col = (
        lax.axis_index("col") * cols - margin + lax.broadcasted_iota(jnp.int32, (1, 1, ext_cols), 2)
    )
    row_inside = (global_row >= 0) & (global_row < total_rows)
    col_inside = (global_col >= 0) & (global_col < total_cols)
    row_step = (global_row >= 0) & (global_row < total_rows - 1)
    col_step = (global_col >= 0) & (global_col < total_cols - 1)
    keep_x = row_step & col_inside
    keep_y = col_step & row_inside
    primal = source
    extra = source
    dual_x = jnp.zeros_like(source)
    dual_y = jnp.zeros_like(source)
    for step in range(ITERS):
        below = jnp.concatenate([extra[:, 1:, :], extra[:, -1:, :]], axis=1)
        right = jnp.concatenate([extra[:, :, 1:], extra[:, :, -1:]], axis=2)
        grad_x = jnp.where(keep_x, below - extra, 0.0)
        grad_y = jnp.where(keep_y, right - extra, 0.0)
        qx = dual_x + dual_step * grad_x
        qy = dual_y + dual_step * grad_y
        local_sum = jnp.sum(qx * qx + qy * qy, axis=0)
        scale = pixel_scale(local_sum, weight)
        dual_x = scale * qx
        dual_y = scale * qy
        above = jnp.concatenate([dual_x[:, :1, :], dual_x[:, :-1, :]], axis=1)
        left = jnp.concatenate([dual_y[:, :, :1], dual_y[:, :, :-1]], axis=2)
        spread = dual_x - above + (dual_y - left)
        newer = (primal + primal_step * spread + primal_step * source) / (1.0 + primal_step)
        extra = 2.0 * newer - primal
        primal = newer
    return primal[:, margin : margin + rows, margin : margin + cols]


def solution(mesh):
    placed = (P("band", "row", "col"), P("row", "col"))
    return jax.shard_map(
        local, mesh=mesh, in_specs=placed, out_specs=P("band", "row", "col"), check_vma=False
    )
```

profile of v0, /device:TPU:63, one launch (start us, length us, event | category | flops | bytes accessed | tf_op | source)
XLA Modules:
  0.0 179.5 jit_solution(8338639192761379242)
XLA Ops:
  0.0 1.8 %pad_maximum_fusion.2 = (f32[29,4,1024]{2,1,0:T(4,128)S(1)}, f32[29,4,1024]{2,1,0:T(4,128)S(1)}) fusion(f32[1,16,1024]{2,1,0:T(8,128)} %bitcast.41, f32[28,16,1024]{2,1,0:T(8,128)} %param.2), kind=kLoop, calls=%fused_computation.78 | loop fusion | flops 237568 | bytes 2850816 | tf_op jit(solution)/shard_map/slice | solution.py:23
  2.1 1.8 collective-permute-start.1
  4.2 1.3 collective-permute-start
  6.2 8.2 %collective-permute-done.1 = f32[29,4,1024]{2,0,1:T(8,128)S(1)} collective-permute-done((f32[29,4,1024]{2,0,1:T(8,128)S(1)}, f32[29,4,1024]{2,0,1:T(8,128)S(1)}, u32[]{:S(2)}, u32[]{:S(2)}) %collective-permute-start.1) | collective-permute-done | bytes 475168 | tf_op jit(solution)/shard_map/ppermute | solution.py:28
  14.8 13.6 %collective-permute-done = f32[29,4,1024]{2,0,1:T(8,128)} collective-permute-done((f32[29,4,1024]{2,0,1:T(8,128)S(1)}, f32[29,4,1024]{2,0,1:T(8,128)}, u32[]{:S(2)}, u32[]{:S(2)}) %collective-permute-start) | collective-permute-done | bytes 475168 | tf_op jit(solution)/shard_map/ppermute | solution.py:26
  28.4 1.3 copy.17
  30.4 2.5 %collective-permute-start.3 = (f32[29,24,4]{2,1,0:T(8,128)S(1)}, f32[29,24,4]{2,1,0:T(8,128)S(1)}, u32[]{:S(2)}, u32[]{:S(2)}) collective-permute-start(f32[29,24,4]{2,1,0:T(8,128)S(1)} %get-tuple-element.23), channel_id=1, source_target_pairs={{8,0},{16,8},{24,16},{9,1},{17,9},{25,17},{10,2},{18,10},{26,18},{... | collective-permute-start | bytes 33416 | tf_op jit(solution)/shard_map/ppermute | solution.py:28
  32.9 1.3 collective-permute-start.2
  34.9 4.1 %collective-permute-done.3 = f32[29,24,4]{2,1,0:T(8,128)S(1)} collective-permute-done((f32[29,24,4]{2,1,0:T(8,128)S(1)}, f32[29,24,4]{2,1,0:T(8,128)S(1)}, u32[]{:S(2)}, u32[]{:S(2)}) %collective-permute-start.3) | collective-permute-done | bytes 11168 | tf_op jit(solution)/shard_map/ppermute | solution.py:28
  39.8 3.2 %collective-permute-done.2 = f32[29,24,4]{2,1,0:T(8,128)} collective-permute-done((f32[29,24,4]{2,1,0:T(8,128)S(1)}, f32[29,24,4]{2,1,0:T(8,128)}, u32[]{:S(2)}, u32[]{:S(2)}) %collective-permute-start.2) | collective-permute-done | bytes 11168 | tf_op jit(solution)/shard_map/ppermute | solution.py:26
  43.0 3.5 %concatenate.59 = f32[29,24,1032]{2,1,0:T(8,128)S(1)} concatenate(f32[29,24,4]{2,1,0:T(8,128)} %collective-permute-done.2, f32[29,24,1024]{2,1,0:T(8,128)} %copy-done.2, f32[29,24,4]{2,1,0:T(8,128)} %copy-done.8), dimensions={2} | concatenate | bytes 5746176 | tf_op jit(solution)/shard_map/concatenate | solution.py:24
  47.7 1.0 copy-done.9
  49.1 1.6 add_reduce_fusion.3
  50.8 22.4 %all-gather = f32[192,1032]{1,0:T(8,128)} all-gather(f32[24,1032]{1,0:T(8,128)S(1)} %add_reduce_fusion.3), channel_id=2, replica_groups=mesh['row'=8,'col'=4,'band'=8] {'band'}, dimensions={0}, use_global_device_ids=true | all-gather | bytes 891648 | tf_op jit(solution)/shard_map/all_gather | solution.py:14
  73.2 1.9 %reduce_sum.73 = f32[24,1032]{1,0:T(8,128)} reduce(f32[8,24,1032]{2,1,0:T(8,128)} %bitcast.38, f32[]{:T(128)} %constant.39.clone.1), dimensions={0}, to_apply=%region_1.2 | reduce | flops 173376 | bytes 891652 | tf_op jit(solution)/shard_map/reduce_sum | solution.py:15
  76.0 3.8 %broadcast_multiply_fusion.6 = (f32[28,24,1032]{2,1,0:T(8,128)S(1)}, f32[28,24,1032]{2,1,0:T(8,128)S(1)}) fusion(f32[24,1032]{1,0:T(8,128)S(1)} %fusion.42, f32[29,24,1032]{2,1,0:T(8,128)S(1)} %concatenate.59, f32[28,24,1]{2,1,0:T(8,128)S(1)} %slice.168, f32[28,24,1031]{2,1,0:T(8,128)} %copy-done, pred[24,1032]{1,0:T(8,128)(4,1)} %broadcast_and_fusion, ...), kind=kLoop, calls=%fused_computation.75 | loop fusion | flops 5548032 | bytes 14018688 | tf_op jit(solution)/shard_map/mul | solution.py:77
  79.9 3.1 %multiply_subtract_fusion.2 = (f32[28,24,1032]{2,1,0:T(8,128)S(1)}, f32[28,24,1032]{2,1,0:T(8,128)}) fusion(f32[29,24,1032]{2,1,0:T(8,128)S(1)} %concatenate.59, f32[28,24,1032]{2,1,0:T(8,128)S(1)} %get-tuple-element.20, f32[28,24,1031]{2,1,0:T(8,128)S(1)} %bitcast.30, f32[28,24,1]{2,1,0:T(8,128)S(1)} %slice.171, f32[28,24,1032]{2,1,0:T(8,128)S(1)} %get-tuple-element.21, ...), kind=kLoop, calls=%fused_computation.55 | loop fusion | flops 7628544 | bytes 19418112 | tf_op jit(solution)/shard_map/sub | solution.py:82
  84.8 3.7 %add_reduce_fusion.2 = (f32[24,1032]{1,0:T(8,128)S(1)}, f32[28,24,1032]{2,1,0:T(8,128)}, f32[28,24,1032]{2,1,0:T(8,128)}) fusion(f32[28,24,1032]{2,1,0:T(8,128)S(1)} %get-tuple-element.21, f32[28,24,1032]{2,1,0:T(8,128)S(1)} %get-tuple-element.18, f32[28,1,1032]{2,1,0:T(1,128)S(1)} %slice.174, f32[28,23,1032]{2,1,0:T(8,128)S(1)} %slice.173, ...), kind=kLoop, calls=%fused_computation.54 | loop fusion | flops 9684288 | bytes 19566720 | tf_op jit(solution)/shard_map/reduce_sum | solution.py:74
  88.5 18.5 %all-gather.1 = f32[192,1032]{1,0:T(8,128)} all-gather(f32[24,1032]{1,0:T(8,128)S(1)} %get-tuple-element.15), channel_id=3, replica_groups=mesh['row'=8,'col'=4,'band'=8] {'band'}, dimensions={0}, use_global_device_ids=true | all-gather | bytes 891648 | tf_op jit(solution)/shard_map/all_gather | solution.py:14
  107.0 1.2 reduce_sum.75
  108.3 3.4 %broadcast_multiply_fusion.4 = (f32[28,24,1032]{2,1,0:T(8,128)S(1)}, f32[28,24,1032]{2,1,0:T(8,128)S(1)}) fusion(f32[28,24,1032]{2,1,0:T(8,128)} %get-tuple-element.17, f32[24,1032]{1,0:T(8,128)S(1)} %fusion.43, f32[28,24,1032]{2,1,0:T(8,128)} %get-tuple-element.16), kind=kLoop, calls=%fused_computation.73 | loop fusion | flops 1387008 | bytes 11195136 | tf_op jit(solution)/shard_map/mul | solution.py:77
  112.0 3.3 %multiply_subtract_fusion.1 = (f32[28,24,1032]{2,1,0:T(8,128)S(1)}, f32[28,24,1032]{2,1,0:T(8,128)}) fusion(f32[28,24,1032]{2,1,0:T(8,128)S(1)} %copy-done.3, f32[29,24,1032]{2,1,0:T(8,128)S(1)} %concatenate.59, f32[28,24,1032]{2,1,0:T(8,128)S(1)} %get-tuple-element.31, f32[28,24,1031]{2,1,0:T(8,128)S(1)} %bitcast.29, f32[28,24,1]{2,1,0:T(8,128)S(1)} %slice.179, ...), kind=kLoop, calls=%fused_computation.53 | loop fusion | flops 8322048 | bytes 22192128 | tf_op jit(solution)/shard_map/sub | solution.py:82
  116.6 3.7 %add_reduce_fusion.1 = (f32[24,1032]{1,0:T(8,128)S(1)}, f32[28,24,1032]{2,1,0:T(8,128)}, f32[28,24,1032]{2,1,0:T(8,128)}) fusion(f32[28,24,1032]{2,1,0:T(8,128)S(1)} %get-tuple-element.32, f32[28,24,1032]{2,1,0:T(8,128)S(1)} %get-tuple-element.13, f32[28,1,1032]{2,1,0:T(1,128)S(1)} %slice.182, f32[28,23,1032]{2,1,0:T(8,128)S(1)} %slice.181, ...), kind=kLoop, calls=%fused_computation.52 | loop fusion | flops 9684288 | bytes 19566720 | tf_op jit(solution)/shard_map/reduce_sum | solution.py:74
  120.3 17.2 %all-gather.2 = f32[192,1032]{1,0:T(8,128)} all-gather(f32[24,1032]{1,0:T(8,128)S(1)} %get-tuple-element.10), channel_id=4, replica_groups=mesh['row'=8,'col'=4,'band'=8] {'band'}, dimensions={0}, use_global_device_ids=true | all-gather | bytes 891648 | tf_op jit(solution)/shard_map/all_gather | solution.py:14
  137.5 1.2 reduce_sum.77
  138.8 3.4 %broadcast_multiply_fusion.2 = (f32[28,24,1032]{2,1,0:T(8,128)S(1)}, f32[28,24,1032]{2,1,0:T(8,128)S(1)}) fusion(f32[28,24,1032]{2,1,0:T(8,128)} %get-tuple-element.12, f32[24,1032]{1,0:T(8,128)S(1)} %fusion.44, f32[28,24,1032]{2,1,0:T(8,128)} %get-tuple-element.11), kind=kLoop, calls=%fused_computation.71 | loop fusion | flops 1387008 | bytes 11195136 | tf_op jit(solution)/shard_map/mul | solution.py:77
  142.5 3.8 %multiply_subtract_fusion = (f32[28,24,1032]{2,1,0:T(8,128)S(1)}, f32[28,24,1032]{2,1,0:T(8,128)}, f32[28,24,1032]{2,1,0:T(8,128)}) fusion(f32[28,24,1032]{2,1,0:T(8,128)S(1)} %copy-done.4, f32[29,24,1032]{2,1,0:T(8,128)S(1)} %concatenate.59, f32[28,24,1032]{2,1,0:T(8,128)S(1)} %get-tuple-element.29, f32[28,24,1031]{2,1,0:T(8,128)S(1)} %bitcast.31, ...), kind=kLoop, calls=%fused_computation.51 | loop fusion | flops 8322048 | bytes 24966144 | tf_op jit(solution)/shard_map/sub | solution.py:82
  147.6 3.7 %add_reduce_fusion = (f32[24,1032]{1,0:T(8,128)S(1)}, f32[28,24,1032]{2,1,0:T(8,128)}, f32[28,24,1032]{2,1,0:T(8,128)}) fusion(f32[28,24,1032]{2,1,0:T(8,128)S(1)} %get-tuple-element.30, f32[28,24,1032]{2,1,0:T(8,128)S(1)} %get-tuple-element.8, f32[28,1,1032]{2,1,0:T(1,128)S(1)} %slice.190, f32[28,23,1032]{2,1,0:T(8,128)S(1)} %slice.189, ...), kind=kLoop, calls=%fused_computation.50 | loop fusion | flops 9684288 | bytes 19566720 | tf_op jit(solution)/shard_map/reduce_sum | solution.py:74
  151.3 16.8 %all-gather.3 = f32[192,1032]{1,0:T(8,128)} all-gather(f32[24,1032]{1,0:T(8,128)S(1)} %get-tuple-element.5), channel_id=5, replica_groups=mesh['row'=8,'col'=4,'band'=8] {'band'}, dimensions={0}, use_global_device_ids=true | all-gather | bytes 891648 | tf_op jit(solution)/shard_map/all_gather | solution.py:14
  168.2 1.2 reduce_sum.79
  169.5 3.4 %broadcast_multiply_fusion.1 = (f32[28,24,1032]{2,1,0:T(8,128)S(1)}, f32[28,24,1032]{2,1,0:T(8,128)S(1)}) fusion(f32[28,24,1032]{2,1,0:T(8,128)} %get-tuple-element.6, f32[24,1032]{1,0:T(8,128)S(1)} %fusion.45, f32[28,24,1032]{2,1,0:T(8,128)} %get-tuple-element.7), kind=kLoop, calls=%fused_computation.70 | loop fusion | flops 1387008 | bytes 11195136 | tf_op jit(solution)/shard_map/mul | solution.py:76
  174.1 5.4 %fusion.38 = f32[28,16,1024]{2,1,0:T(8,128)} fusion(f32[28,24,1]{2,1,0:T(8,128)S(1)} %slice.195, f32[28,24,1031]{2,1,0:T(8,128)S(1)} %bitcast.35, f32[28,1,1032]{2,1,0:T(1,128)S(1)} %slice.193, f32[28,23,1032]{2,1,0:T(8,128)S(1)} %bitcast.36, f32[28,24,1032]{2,1,0:T(8,128)S(1)} %copy-done.6, f32[28,24,1032]{2,1,0:T(8,128)S(1)} %copy-done.5, ...), kind=kLoop, calls=%fused_computation.65 | loop fusion | flops 4587520 | bytes 14723072 | tf_op jit(solution)/shard_map/div | solution.py:81
  (68 shorter events, 13.0 us)
Async XLA Ops:
  0.0 29.7 %copy-start.7 = (f32[28,16,1024]{2,1,0:T(8,128)S(1)}, f32[28,16,1024]{2,1,0:T(8,128)}, u32[]{:S(2)}) copy-start(f32[28,16,1024]{2,1,0:T(8,128)} %param.2) | copy-start | bytes 5505028
  0.0 29.7 %copy-start.15 = (f32[16,1024]{1,0:T(8,128)S(1)}, f32[16,1024]{1,0:T(8,128)}, u32[]{:S(2)}) copy-start(f32[16,1024]{1,0:T(8,128)} %param.3) | copy-start | bytes 196612
  2.1 12.3 %collective-permute-start.1 = (f32[29,4,1024]{2,0,1:T(8,128)S(1)}, f32[29,4,1024]{2,0,1:T(8,128)S(1)}, u32[]{:S(2)}, u32[]{:S(2)}) collective-permute-start(f32[29,4,1024]{2,0,1:T(8,128)S(1)} %copy.16), channel_id=1, source_target_pairs={{32,0},{64,32},{96,64},{128,96},{160,128},{192,160},{224,192},{33,... | collective-permute-start | bytes 1425416 | tf_op jit(solution)/shard_map/ppermute | solution.py:28
  4.2 24.2 %collective-permute-start = (f32[29,4,1024]{2,0,1:T(8,128)S(1)}, f32[29,4,1024]{2,0,1:T(8,128)}, u32[]{:S(2)}, u32[]{:S(2)}) collective-permute-start(f32[29,4,1024]{2,0,1:T(8,128)S(1)} %copy.15), channel_id=1, source_target_pairs={{0,32},{32,64},{64,96},{96,128},{128,160},{160,192},{192,224},{1,3... | collective-permute-start | bytes 1425416 | tf_op jit(solution)/shard_map/ppermute | solution.py:26
  30.2 8.8 %copy-start.2 = (f32[29,24,1024]{2,1,0:T(8,128)}, f32[29,24,1024]{2,1,0:T(8,128)S(1)}, u32[]{:S(2)}) copy-start(f32[29,24,1024]{2,1,0:T(8,128)S(1)} %pad_maximum_fusion) | copy-start | bytes 8552452
  30.4 8.6 %collective-permute-start.3 = (f32[29,24,4]{2,1,0:T(8,128)S(1)}, f32[29,24,4]{2,1,0:T(8,128)S(1)}, u32[]{:S(2)}, u32[]{:S(2)}) collective-permute-start(f32[29,24,4]{2,1,0:T(8,128)S(1)} %get-tuple-element.23), channel_id=1, source_target_pairs={{8,0},{16,8},{24,16},{9,1},{17,9},{25,17},{10,2},{18,10},{26,18},{... | collective-permute-start | bytes 33416 | tf_op jit(solution)/shard_map/ppermute | solution.py:28
  32.9 10.1 %collective-permute-start.2 = (f32[29,24,4]{2,1,0:T(8,128)S(1)}, f32[29,24,4]{2,1,0:T(8,128)}, u32[]{:S(2)}, u32[]{:S(2)}) collective-permute-start(f32[29,24,4]{2,1,0:T(8,128)S(1)} %get-tuple-element.24), channel_id=1, source_target_pairs={{0,8},{8,16},{16,24},{1,9},{9,17},{17,25},{2,10},{10,18},{18,26},{... | collective-permute-start | bytes 33416 | tf_op jit(solution)/shard_map/ppermute | solution.py:26
  39.0 0.7 copy-start.8
  46.6 2.3 %copy-start.10 = (f32[28,1,1032]{2,1,0:T(1,128)}, f32[28,1,1032]{2,1,0:T(1,128)S(1)}, u32[]{:S(2)}) copy-start(f32[28,1,1032]{2,1,0:T(1,128)S(1)} %slice.165) | copy-start | bytes 346756
  47.5 1.6 copy-start
  47.5 1.2 copy-start.9
  47.5 1.6 copy-start.11
  47.5 1.6 copy-start.13
  48.7 2.1 %copy-start.1 = (f32[28,23,1032]{2,1,0:T(8,128)}, f32[28,23,1032]{2,1,0:T(8,128)S(1)}, u32[]{:S(2)}) copy-start(f32[28,23,1032]{2,1,0:T(8,128)S(1)} %slice.164) | copy-start | bytes 7975300
  84.1 0.8 copy-start.12
  84.1 0.8 copy-start.14
  108.3 3.7 %copy-start.3 = (f32[28,24,1032]{2,1,0:T(8,128)S(1)}, f32[28,24,1032]{2,1,0:T(8,128)}, u32[]{:S(2)}) copy-start(f32[28,24,1032]{2,1,0:T(8,128)} %get-tuple-element.19) | copy-start | bytes 8322052
  138.8 3.7 %copy-start.4 = (f32[28,24,1032]{2,1,0:T(8,128)S(1)}, f32[28,24,1032]{2,1,0:T(8,128)}, u32[]{:S(2)}) copy-start(f32[28,24,1032]{2,1,0:T(8,128)} %get-tuple-element.14) | copy-start | bytes 8322052
  169.5 3.7 %copy-start.5 = (f32[28,24,1032]{2,1,0:T(8,128)S(1)}, f32[28,24,1032]{2,1,0:T(8,128)}, u32[]{:S(2)}) copy-start(f32[28,24,1032]{2,1,0:T(8,128)} %get-tuple-element.9) | copy-start | bytes 8322052
  169.5 4.6 %copy-start.6 = (f32[28,24,1032]{2,1,0:T(8,128)S(1)}, f32[28,24,1032]{2,1,0:T(8,128)}, u32[]{:S(2)}) copy-start(f32[28,24,1032]{2,1,0:T(8,128)} %get-tuple-element.22) | copy-start | bytes 8322052
where the time goes:
time: 180 us
  blocking collectives  74.9 us (42%)
  other arithmetic  52.5 us (29%)
  waiting for transfers between devices  29.1 us (16%)
  local copies, waits for them, and re-layouts  15.7 us (9%)
  starting transfers between devices  6.82 us (4%)
    all_gather x4, blocking collectives, over_pieces(): blocks = lax.all_gather(shard, axis)  74.9 us
    ppermute x2, waiting for transfers between devices, with_halo(): lax.ppermute(tail, axis, [(i, (i + 1) % count) for i in range(ends)])  16.8 us
    reduce_sum x4, other arithmetic, local(): local_sum = jnp.sum(qx * qx + qy * qy, axis=0)  12.7 us
    ppermute x2, waiting for transfers between devices, with_halo(): lax.ppermute(head, axis, [((i + 1) % count, i) for i in range(ends)])  12.3 us
    mul x3, other arithmetic, local(): dual_y = scale * qy  10.5 us
    sub x3, other arithmetic, local(): extra = 2.0 * newer - primal  10.1 us
    reduce_sum x4, other arithmetic, over_pieces(): return blocks.sum(axis=0)  5.54 us
    div x1, other arithmetic, local(): (primal + primal_step * spread + primal_step * source) / (1.0 + primal_step)  5.42 us
  transfers between devices with their start and end apart: 4, of which 4 were waited for; matrix products, arithmetic and copies ran while one was open for 1% of the time, Pallas kernels for 0%

commit v1 on v0

v1 whole, which is shorter than its diff:
```python
import functools

import jax
import jax.numpy as jnp
from jax import lax
from jax.experimental import pallas as pl
from jax.experimental.pallas import tpu as pltpu
from jax.sharding import PartitionSpec as P

MESH = pl.DeviceIdType.MESH
ITERS = 4
SIGMA = 0.35
TAU = 0.35
C0 = 1.0 / (1.0 + TAU)
KAPPA = TAU / (1.0 + TAU)
M = 4
LANES = 128
RPAD = 8
SROWS = 32
F32 = jnp.float32


def kernel(dims, noisy_ref, weight_ref, out_ref, N, U, UB, PX, PY, QX, QY, SC, MX, MY, OUT,
           PL, PR, RL, RR, SB, RB1, TB, RB2,
           s_in, s_w, sw_s, sw_r, rh_s, rh_r, st_s, st_r, co_s, co_r, ar_s, ar_r, o_l, o_s, o_r):
    nrow, ncol, nband = dims
    bands, rows, cols = noisy_ref.shape
    NB = 2 * bands
    half = cols // 2
    CT = half // LANES
    row = lax.axis_index("row")
    col = lax.axis_index("col")
    band = lax.axis_index("band")
    zc = nband // 2
    z = band // 2
    core = band % 2
    g = col * 2 + core
    ng = ncol * 2

    def dev(r=None, gc=None, zz=None):
        rr = row if r is None else (row + r + nrow) % nrow
        gg = g if gc is None else (g + gc + ng) % ng
        zz = z if zz is None else zz
        return {"row": rr, "col": gg // 2, "band": zz * 2 + gg % 2}

    partner = {"row": row, "col": col, "band": z * 2 + 1 - core}
    up, down, left, right = dev(r=-1), dev(r=1), dev(gc=-1), dev(gc=1)
    corners = (dev(-1, -1), dev(-1, 1), dev(1, -1), dev(1, 1))
    zA = dev(zz=z + 1 - 2 * (z % 2))
    zB = dev(zz=zc - 1 - z)

    loads = []
    for c in range(CT):
        src = noisy_ref.at[:, :, pl.ds(pl.multiple_of(core * half + c * LANES, LANES), LANES)]
        dst = N.at[c, pl.ds(core * bands, bands), RPAD : RPAD + rows, :]
        loads.append(pltpu.make_async_copy(src, dst, s_in.at[c]))
        wsrc = weight_ref.at[:, pl.ds(pl.multiple_of(core * half + c * LANES, LANES), LANES)]
        loads.append(pltpu.make_async_copy(wsrc, N.at[c, NB, RPAD : RPAD + rows, :], s_w.at[c]))
    for cp in loads:
        cp.start()

    barrier = pltpu.get_barrier_semaphore()
    peers = (partner, up, down, left, right, zA, zB) + corners
    for d in peers:
        pl.semaphore_signal(barrier, inc=1, device_id=d, device_id_type=MESH)
    pl.semaphore_wait(barrier, len(peers))

    def remote(src, dst, ss, rs, d):
        return pltpu.make_async_remote_copy(
            src_ref=src, dst_ref=dst, send_sem=ss, recv_sem=rs, device_id=d, device_id_type=MESH
        )

    swaps = []
    for c in range(CT):
        src = noisy_ref.at[:, :, pl.ds(pl.multiple_of((1 - core) * half + c * LANES, LANES), LANES)]
        dst = N.at[c, pl.ds(core * bands, bands), RPAD : RPAD + rows, :]
        swaps.append(remote(src, dst, sw_s.at[c], sw_r.at[c], partner))
    for cp in swaps:
        cp.start()

    lane = lax.broadcasted_iota(jnp.int32, (8, LANES), 1)
    sub = lax.broadcasted_iota(jnp.int32, (8, LANES), 0)
    coef = KAPPA * SIGMA
    for k in range(3):
        for c in range(CT + 1):
            grow = row * rows + (k * 8 - M) + sub
            if c < CT:
                gcol = g * half + c * LANES + lane
            else:
                gcol = g * half + jnp.where(lane < LANES // 2, half + lane, lane - LANES)
            rin = (grow >= 0) & (grow < nrow * rows)
            cin = (gcol >= 0) & (gcol < ng * half)
            kx = (grow >= 0) & (grow < nrow * rows - 1) & cin
            ky = (gcol >= 0) & (gcol < ng * half - 1) & rin
            MX[k, c] = jnp.where(kx, coef, 0.0).astype(F32)
            MY[k, c] = jnp.where(ky, coef, 0.0).astype(F32)

    for cp in loads:
        cp.wait()
    for cp in swaps:
        cp.wait_recv()

    rowh = (
        remote(N.at[0:CT, :, RPAD : RPAD + M, :], N.at[0:CT, :, RPAD + rows : RPAD + rows + M, :], rh_s.at[0], rh_r.at[0], up),
        remote(N.at[0:CT, :, RPAD + rows - M : RPAD + rows, :], N.at[0:CT, :, RPAD - M : RPAD, :], rh_s.at[1], rh_r.at[1], down),
    )
    for cp in rowh:
        cp.start()

    G = 128 // M
    for gi in range(2):
        cnt = min(G, NB + 1 - gi * G)

        def pack(e, acc):
            here = (lane >= e * M) & (lane < e * M + M)
            out = []
            for h in range(2):
                a = N[0, gi * G + e, RPAD + 8 * h : RPAD + 8 * h + 8, :]
                b = N[CT - 1, gi * G + e, RPAD + 8 * h : RPAD + 8 * h + 8, :]
                out.append(jnp.where(here, pltpu.roll(a, e * M, 1), acc[2 * h]))
                out.append(jnp.where(here, pltpu.roll(b, e * M + M, 1), acc[2 * h + 1]))
            return tuple(out)

        zero = jnp.zeros((8, LANES), F32)
        acc = lax.fori_loop(0, cnt, pack, (zero,) * 4)
        for h in range(2):
            PL[gi, 8 * h : 8 * h + 8, :] = acc[2 * h]
            PR[gi, 8 * h : 8 * h + 8, :] = acc[2 * h + 1]

    lo, hi = slice(RPAD, RPAD + rows), RPAD + rows
    strips = [
        remote(PL, RR.at[:, lo, :], st_s.at[0], st_r.at[0], left),
        remote(PR, RL.at[:, lo, :], st_s.at[1], st_r.at[1], right),
        remote(PL.at[:, 0:M, :], RR.at[:, hi : hi + M, :], co_s.at[0], co_r.at[0], corners[0]),
        remote(PR.at[:, 0:M, :], RL.at[:, hi : hi + M, :], co_s.at[1], co_r.at[1], corners[1]),
        remote(PL.at[:, rows - M : rows, :], RR.at[:, RPAD - M : RPAD, :], co_s.at[2], co_r.at[2], corners[2]),
        remote(PR.at[:, rows - M : rows, :], RL.at[:, RPAD - M : RPAD, :], co_s.at[3], co_r.at[3], corners[3]),
    ]
    for cp in strips:
        cp.start()
    for cp in strips:
        cp.wait_recv()
    for gi in range(2):
        cnt = min(G, NB + 1 - gi * G)

        def unpack(e, carry):
            for k in range(3):
                r = RR[gi, RPAD - M + 8 * k : RPAD - M + 8 * k + 8, :]
                l = RL[gi, RPAD - M + 8 * k : RPAD - M + 8 * k + 8, :]
                v = jnp.where(
                    lane < LANES // 2,
                    pltpu.roll(r, (LANES - e * M) % LANES, 1),
                    pltpu.roll(l, LANES - M - e * M, 1),
                )
                N[CT, gi * G + e, RPAD - M + 8 * k : RPAD - M + 8 * k + 8, :] = v
            return carry

        lax.fori_loop(0, cnt, unpack, 0)
    for cp in rowh:
        cp.wait_recv()

    first = lane == 0
    last = lane == LANES - 1
    C = CT + 1

    def rowslice(k, off=0):
        return slice(RPAD - M + 8 * k + off, RPAD - M + 8 * k + 8 + off)

    def dual(it, k):
        src = N if it == 0 else UB
        mx = [MX[k, c] for c in range(C)]
        my = [MY[k, c] for c in range(C)]

        def body(b, acc):
            ub = [src[c, b, rowslice(k), :] for c in range(C)]
            rolled = [pltpu.roll(v, LANES - 1, 1) for v in ub]
            out = []
            for c in range(C):
                below = src[c, b, rowslice(k, 1), :]
                rightv = jnp.where(last, rolled[(c + 1) % C], rolled[c])
                qx = mx[c] * (below - ub[c])
                qy = my[c] * (rightv - ub[c])
                if it > 0:
                    qx = qx + PX[c, b, rowslice(k), :]
                    qy = qy + PY[c, b, rowslice(k), :]
                QX[c, b, rowslice(k), :] = qx
                QY[c, b, rowslice(k), :] = qy
                out.append(acc[c] + (qx * qx + qy * qy))
            return tuple(out)

        acc = lax.fori_loop(0, NB, body, (jnp.zeros((8, LANES), F32),) * C, unroll=2)
        for c in range(C):
            SB[it, k * C + c] = acc[c]

    def primal(it, k):
        sc = [SC[c, rowslice(k), :] for c in range(C)]
        scu = [SC[c, rowslice(k, -1), :] for c in range(C)]

        def body(b, carry):
            py = [sc[c] * QY[c, b, rowslice(k), :] for c in range(C)]
            rolled = [pltpu.roll(v, 1, 1) for v in py]
            for c in range(C):
                px = sc[c] * QX[c, b, rowslice(k), :]
                pxu = scu[c] * QX[c, b, rowslice(k, -1), :]
                pyl = jnp.where(first, rolled[(c - 1) % C], rolled[c])
                div = (px - pxu) + (py[c] - pyl)
                n = N[c, b, rowslice(k), :]
                if it == 0:
                    old = n
                    new = n + div
                else:
                    old = U[c, b, rowslice(k), :]
                    new = C0 * old + (KAPPA * n + div)
                PX[c, b, rowslice(k), :] = px
                PY[c, b, rowslice(k), :] = py[c]
                U[c, b, rowslice(k), :] = new
                UB[c, b, rowslice(k), :] = 2.0 * new - old
            return carry

        lax.fori_loop(0, NB, body, 0, unroll=2)

    def final(k):
        here = slice(RPAD + 8 * k, RPAD + 8 * k + 8)
        above = slice(RPAD + 8 * k - 1, RPAD + 8 * k + 7)
        sc = [SC[c, here, :] for c in range(C)]
        scu = [SC[c, above, :] for c in range(C)]

        def body(b, carry):
            py = [sc[c] * QY[c, b, here, :] for c in range(C)]
            rolled = [pltpu.roll(v, 1, 1) for v in py]
            for c in range(CT):
                px = sc[c] * QX[c, b, here, :]
                pxu = scu[c] * QX[c, b, above, :]
                pyl = jnp.where(first, rolled[(c - 1) % C], rolled[c])
                div = (px - pxu) + (py[c] - pyl)
                OUT[c, b, 8 * k : 8 * k + 8, :] = C0 * U[c, b, here, :] + (KAPPA * N[c, b, here, :] + div)
            return carry

        lax.fori_loop(0, NB, body, 0, unroll=2)

    def scales(it, t0, t1):
        for t in range(t0, t1):
            k, c = divmod(t, C)
            w = N[c, NB, rowslice(k), :]
            s = TB[it, t] + RB2[it, t]
            SC[c, rowslice(k), :] = w / jnp.maximum(w, jnp.sqrt(1.0 + s * (1.0 / (KAPPA * KAPPA))))

    T = 3 * C
    H = 8
    parts = ((0, H), (H, T))
    inflight = []
    for it in range(ITERS):
        def step1(h):
            a, b = parts[h]
            return remote(SB.at[it, a:b], RB1.at[it, a:b], ar_s.at[it, 0, h], ar_r.at[it, 0, h], (zA, zB)[h])

        def step2(h):
            a, b = parts[h]
            return remote(TB.at[it, a:b], RB2.at[it, a:b], ar_s.at[it, 1, h], ar_r.at[it, 1, h], (zB, zA)[h])

        first_copies = [step1(0), step1(1)]
        second_copies = [step2(0), step2(1)]
        dual(it, 0)
        dual(it, 1)
        first_copies[0].start()
        dual(it, 2)
        first_copies[1].start()
        for h in range(2):
            first_copies[h].wait_recv()
            a, b = parts[h]
            for t in range(a, b):
                TB[it, t] = SB[it, t] + RB1[it, t]
            second_copies[h].start()
        second_copies[0].wait_recv()
        scales(it, *parts[0])
        second_copies[1].wait_recv()
        scales(it, *parts[1])
        inflight += first_copies + second_copies
        if it < ITERS - 1:
            for k in range(3):
                primal(it, k)
        else:
            for k in range(2):
                final(k)

    outs = []
    for c in range(CT):
        osrc = OUT.at[c, pl.ds(core * bands, bands)]
        lanes = pl.ds(pl.multiple_of(core * half + c * LANES, LANES), LANES)
        outs.append(pltpu.make_async_copy(osrc, out_ref.at[:, :, lanes], o_l.at[c]))
        osrc = OUT.at[c, pl.ds((1 - core) * bands, bands)]
        outs.append(remote(osrc, out_ref.at[:, :, lanes], o_s.at[c], o_r.at[c], partner))
    for cp in outs:
        cp.start()
    for cp in swaps + list(rowh) + strips + inflight:
        cp.wait_send()
    for cp in outs:
        cp.wait()


def solution(mesh):
    dims = tuple(mesh.shape[a] for a in ("row", "col", "band"))

    def local(noisy, weight_map):
        bands, rows, cols = noisy.shape
        NB = 2 * bands
        CT = cols // 2 // LANES
        C = CT + 1
        vm = lambda *s: pltpu.VMEM(s, F32)
        big = lambda n=NB: vm(C, n, SROWS, LANES)
        dma = lambda *s: pltpu.SemaphoreType.DMA(s)
        return pl.pallas_call(
            functools.partial(kernel, dims),
            out_shape=jax.ShapeDtypeStruct(noisy.shape, F32),
            in_specs=[pl.BlockSpec(memory_space=pl.ANY)] * 2,
            out_specs=pl.BlockSpec(memory_space=pl.ANY),
            scratch_shapes=[
                big(NB + 1), big(), big(), big(), big(), big(), big(),
                vm(C, SROWS, LANES), vm(3, C, 8, LANES), vm(3, C, 8, LANES), vm(CT, NB, rows, LANES),
                vm(2, rows, LANES), vm(2, rows, LANES), vm(2, SROWS, LANES), vm(2, SROWS, LANES),
                vm(ITERS, 16, 8, LANES), vm(ITERS, 16, 8, LANES), vm(ITERS, 16, 8, LANES), vm(ITERS, 16, 8, LANES),
                dma(CT), dma(CT), dma(CT), dma(CT), dma(2), dma(2), dma(2), dma(2), dma(4), dma(4),
                dma(ITERS, 2, 2), dma(ITERS, 2, 2), dma(CT), dma(CT), dma(CT),
            ],
            compiler_params=pltpu.CompilerParams(
                collective_id=0, has_side_effects=True, vmem_limit_bytes=60 * 1024 * 1024
            ),
        )(noisy, weight_map)

    return jax.shard_map(
        local, mesh=mesh, in_specs=(P("band", "row", "col"), P("row", "col")),
        out_specs=P("band", "row", "col"), check_vma=False,
    )
```

time: 180 us -> 134 us (0.74)
  the two profiles are of different devices: /device:TPU:63 before, /device:TPU:1 now
where the time goes in v1:
time: 134 us
  Pallas kernels  131 us (98%)
  local copies, waits for them, and re-layouts  2.94 us (2%)
    pallas_call x1, Pallas kernels, local(): pl.pallas_call(functools.partial(kernel, dims), out_shape=jax.ShapeDtypeS...  131 us
    unnamed x1, local copies, waits for them, and re-layouts  2.94 us

profile of v1, /device:TPU:1, one launch (start us, length us, event | category | flops | bytes accessed | tf_op | source)
XLA Modules:
  0.0 133.6 jit_solution(15257977473076665962)
XLA Ops:
  0.0 130.6 %shard_map.28 = f32[28,16,1024]{2,1,0:T(8,128)} custom-call(f32[28,16,1024]{2,1,0:T(8,128)} %noisy_ref.1, f32[16,1024]{1,0:T(8,128)} %weight_ref.1), custom_call_target="tpu_custom_call" | custom-call | tf_op jit(solution)/shard_map/pallas_call | solution.py:312
  130.6 2.9 %copy.4 = f32[28,16,1024]{2,1,0:T(8,128)} copy(f32[28,16,1024]{2,1,0:T(8,128)} %shard_map.28) | data formatting | bytes 3670016

commit v2 on v1

--- a/solution.py
+++ b/solution.py
@@ -16,7 +16,7 @@
 M = 4
 LANES = 128
 RPAD = 8
-SROWS = 32
+SROWS = 40
 F32 = jnp.float32
 
 
@@ -100,13 +100,6 @@
     for cp in swaps:
         cp.wait_recv()
 
-    rowh = (
-        remote(N.at[0:CT, :, RPAD : RPAD + M, :], N.at[0:CT, :, RPAD + rows : RPAD + rows + M, :], rh_s.at[0], rh_r.at[0], up),
-        remote(N.at[0:CT, :, RPAD + rows - M : RPAD + rows, :], N.at[0:CT, :, RPAD - M : RPAD, :], rh_s.at[1], rh_r.at[1], down),
-    )
-    for cp in rowh:
-        cp.start()
-
     G = 128 // M
     for gi in range(2):
         cnt = min(G, NB + 1 - gi * G)
@@ -122,7 +115,7 @@
             return tuple(out)
 
         zero = jnp.zeros((8, LANES), F32)
-        acc = lax.fori_loop(0, cnt, pack, (zero,) * 4)
+        acc = lax.fori_loop(0, cnt, pack, (zero,) * 4, unroll=cnt)
         for h in range(2):
             PL[gi, 8 * h : 8 * h + 8, :] = acc[2 * h]
             PR[gi, 8 * h : 8 * h + 8, :] = acc[2 * h + 1]
@@ -138,6 +131,13 @@
     ]
     for cp in strips:
         cp.start()
+    rowh = (
+        remote(N.at[0:CT, :, RPAD : RPAD + M, :], N.at[0:CT, :, RPAD + rows : RPAD + rows + M, :], rh_s.at[0], rh_r.at[0], up),
+        remote(N.at[0:CT, :, RPAD + rows - M : RPAD + rows, :], N.at[0:CT, :, RPAD - M : RPAD, :], rh_s.at[1], rh_r.at[1], down),
+    )
+    for cp in rowh:
+        cp.start()
+
     for cp in strips:
         cp.wait_recv()
     for gi in range(2):
@@ -155,7 +155,7 @@
                 N[CT, gi * G + e, RPAD - M + 8 * k : RPAD - M + 8 * k + 8, :] = v
             return carry
 
-        lax.fori_loop(0, cnt, unpack, 0)
+        lax.fori_loop(0, cnt, unpack, 0, unroll=cnt)
     for cp in rowh:
         cp.wait_recv()
 
@@ -188,7 +188,7 @@
                 out.append(acc[c] + (qx * qx + qy * qy))
             return tuple(out)
 
-        acc = lax.fori_loop(0, NB, body, (jnp.zeros((8, LANES), F32),) * C, unroll=2)
+        acc = lax.fori_loop(0, NB, body, (jnp.zeros((8, LANES), F32),) * C, unroll=14)
         for c in range(C):
             SB[it, k * C + c] = acc[c]
 
@@ -217,7 +217,7 @@
                 UB[c, b, rowslice(k), :] = 2.0 * new - old
             return carry
 
-        lax.fori_loop(0, NB, body, 0, unroll=2)
+        lax.fori_loop(0, NB, body, 0, unroll=14)
 
     def final(k):
         here = slice(RPAD + 8 * k, RPAD + 8 * k + 8)
@@ -236,7 +236,7 @@
                 OUT[c, b, 8 * k : 8 * k + 8, :] = C0 * U[c, b, here, :] + (KAPPA * N[c, b, here, :] + div)
             return carry
 
-        lax.fori_loop(0, NB, body, 0, unroll=2)
+        lax.fori_loop(0, NB, body, 0, unroll=14)
 
     def scales(it, t0, t1):
         for t in range(t0, t1):
@@ -307,7 +307,7 @@
         CT = cols // 2 // LANES
         C = CT + 1
         vm = lambda *s: pltpu.VMEM(s, F32)
-        big = lambda n=NB: vm(C, n, SROWS, LANES)
+        big = lambda: vm(C, NB + 1, SROWS, LANES)
         dma = lambda *s: pltpu.SemaphoreType.DMA(s)
         return pl.pallas_call(
             functools.partial(kernel, dims),
@@ -315,7 +315,7 @@
             in_specs=[pl.BlockSpec(memory_space=pl.ANY)] * 2,
             out_specs=pl.BlockSpec(memory_space=pl.ANY),
             scratch_shapes=[
-                big(NB + 1), big(), big(), big(), big(), big(), big(),
+                big(), big(), big(), big(), big(), big(), big(),
                 vm(C, SROWS, LANES), vm(3, C, 8, LANES), vm(3, C, 8, LANES), vm(CT, NB, rows, LANES),
                 vm(2, rows, LANES), vm(2, rows, LANES), vm(2, SROWS, LANES), vm(2, SROWS, LANES),
                 vm(ITERS, 16, 8, LANES), vm(ITERS, 16, 8, LANES), vm(ITERS, 16, 8, LANES), vm(ITERS, 16, 8, LANES),

time: 134 us -> 88.7 us (0.66)
  Pallas kernels: 131 us -> 85.7 us
    pallas_call x1, Pallas kernels: 131 us -> 85.7 us  [local(): pl.pallas_call(functools.partial(kernel, dims), out_shape=jax.ShapeDtypeS...]
where the time goes in v2:
time: 88.7 us; the launch traced here: 88.6 us
  Pallas kernels  85.7 us (97%)
  local copies, waits for them, and re-layouts  2.94 us (3%)
    pallas_call x1, Pallas kernels, local(): pl.pallas_call(functools.partial(kernel, dims), out_shape=jax.ShapeDtypeS...  85.7 us
    unnamed x1, local copies, waits for them, and re-layouts  2.94 us

profile of v2, /device:TPU:1, one launch (start us, length us, event | category | flops | bytes accessed | tf_op | source)
XLA Modules:
  0.0 88.6 jit_solution(328633177644364313)
XLA Ops:
  0.0 85.7 %shard_map.28 = f32[28,16,1024]{2,1,0:T(8,128)} custom-call(f32[28,16,1024]{2,1,0:T(8,128)} %noisy_ref.1, f32[16,1024]{1,0:T(8,128)} %weight_ref.1), custom_call_target="tpu_custom_call" | custom-call | tf_op jit(solution)/shard_map/pallas_call | solution.py:312
  85.7 2.9 %copy.4 = f32[28,16,1024]{2,1,0:T(8,128)} copy(f32[28,16,1024]{2,1,0:T(8,128)} %shard_map.28) | data formatting | bytes 3670016

commit v3 on v2

v3 whole, which is shorter than its diff:
```python
import functools

import jax
import jax.numpy as jnp
from jax import lax
from jax.experimental import pallas as pl
from jax.experimental.pallas import tpu as pltpu
from jax.sharding import PartitionSpec as P

MESH = pl.DeviceIdType.MESH
ITERS = 4
SIGMA = 0.35
TAU = 0.35
C0 = 1.0 / (1.0 + TAU)
KAPPA = TAU / (1.0 + TAU)
M = 4
LANES = 128
F32 = jnp.float32
O0, O1, T2 = 8, 16, 24
SROWS = 40
UNROLL_B = 14
UNROLL_A = 14


def kernel(dims, noisy_ref, weight_ref, out_ref, N, N2, U, UB, PX, PY, QX, QY, SC, ELO, EUP, MX, MY, OUT,
           PL, PR, RL, RR, SB, RB1, TB, RB2,
           s_in, s_w, sw_s, sw_r, g_s, g_r, rh_s, rh_r, st_s, st_r, ar_s, ar_r, e_s, e_r, o_s, o_r):
    nrow, ncol, nband = dims
    bands, rows, cols = noisy_ref.shape
    NB = 2 * bands
    half = cols // 2
    CT = half // LANES
    C = CT + 1
    row = lax.axis_index("row")
    col = lax.axis_index("col")
    band = lax.axis_index("band")
    zc = nband // 2
    z = band // 2
    core = band % 2
    g = col * 2 + core
    ng = ncol * 2

    def dev(r=0, gc=None, zz=None):
        rr = (row + r + nrow) % nrow
        gg = g if gc is None else (gc + ng) % ng
        zz = z if zz is None else zz
        return {"row": rr, "col": gg // 2, "band": zz * 2 + gg % 2}

    partner = {"row": row, "col": col, "band": z * 2 + 1 - core}
    up, down, left, right = dev(-1), dev(1), dev(0, g - 1), dev(0, g + 1)
    corners = (dev(-1, g - 1), dev(-1, g + 1), dev(1, g - 1), dev(1, g + 1))
    iA, iB = z + 1 - 2 * (z % 2), zc - 1 - z
    zA, zB = dev(zz=iA), dev(zz=iB)
    up_zB, down_zA, up_zA, down_zB = dev(-1, zz=iB), dev(1, zz=iA), dev(-1, zz=iA), dev(1, zz=iB)
    mine = pl.ds(core * bands, bands)

    def lanes_of(t, c):
        return pl.ds(pl.multiple_of(t * half + c * LANES, LANES), LANES)

    barrier = pltpu.get_barrier_semaphore()
    peers = (up_zB, down_zA, up_zA, down_zB) + corners + (up, down, zA, zB, left, right)
    for d in peers:
        pl.semaphore_signal(barrier, inc=1, device_id=d, device_id_type=MESH)

    loads = []
    for c in range(CT):
        loads.append(pltpu.make_async_copy(noisy_ref.at[:, :, lanes_of(core, c)], N.at[c, mine, 8 : 8 + rows, :], s_in.at[c]))
        loads.append(pltpu.make_async_copy(weight_ref.at[:, lanes_of(core, c)], N.at[c, NB, 8 : 8 + rows, :], s_w.at[c]))
    for cp in loads:
        cp.start()

    lane = lax.broadcasted_iota(jnp.int32, (8, LANES), 1)
    sub = lax.broadcasted_iota(jnp.int32, (8, LANES), 0)
    coef = KAPPA * SIGMA
    for k in range(3):
        for c in range(C):
            grow = row * rows + (8 * k + sub if k < 2 else jnp.where(sub < M, rows + sub, sub - 8))
            if c < CT:
                gcol = g * half + c * LANES + lane
            else:
                gcol = g * half + jnp.where(lane < LANES // 2, half + lane, lane - LANES)
            rin = (grow >= 0) & (grow < nrow * rows)
            cin = (gcol >= 0) & (gcol < ng * half)
            kx = (grow >= 0) & (grow < nrow * rows - 1) & cin
            ky = (gcol >= 0) & (gcol < ng * half - 1) & rin
            MX[k, c] = jnp.where(kx, coef, 0.0).astype(F32)
            MY[k, c] = jnp.where(ky, coef, 0.0).astype(F32)

    pl.semaphore_wait(barrier, len(peers))

    def remote(src, dst, ss, rs, d):
        return pltpu.make_async_remote_copy(
            src_ref=src, dst_ref=dst, send_sem=ss, recv_sem=rs, device_id=d, device_id_type=MESH
        )

    swaps = []
    for c in range(CT):
        swaps.append(remote(noisy_ref.at[:, :, lanes_of(1 - core, c)], N.at[c, mine, 8 : 8 + rows, :], sw_s.at[c], sw_r.at[c], partner))
    for cp in swaps:
        cp.start()

    def below_piece(t, c):
        return remote(noisy_ref.at[:, 0:1, lanes_of(t, c)], N.at[c, mine, T2 : T2 + 1, :],
                      g_s.at[t, c], g_r.at[core, c], dev(-1, col * 2 + t))

    def below_arrival(t, c):
        at = N.at[c, pl.ds(t * bands, bands), T2 : T2 + 1, :]
        return remote(at, at, g_s.at[t, c], g_r.at[t, c], partner)

    below = [below_piece(t, c) for c in range(CT) for t in range(2)]
    for cp in below:
        cp.start()

    def margin(i, src0, dst, to):
        return remote(N.at[0:CT, 0:NB, 8 + src0[0] : 8 + src0[1], :], dst, rh_s.at[i], rh_r.at[i], to)

    margins = [
        margin(0, (rows - 1, rows), N.at[0:CT, 0:NB, T2 + 7 : T2 + 8, :], down),
        margin(1, (1, 2), N.at[0:CT, 0:NB, T2 + 1 : T2 + 2, :], up),
        margin(2, (rows - 2, rows - 1), N.at[0:CT, 0:NB, T2 + 6 : T2 + 7, :], down),
        margin(3, (2, 4), N2.at[:, :, 2:4, :], up),
        margin(4, (rows - 4, rows - 2), N2.at[:, :, 4:6, :], down),
        remote(N.at[0:CT, NB, 8 : 8 + M, :], N.at[0:CT, NB, T2 : T2 + M, :], rh_s.at[5], rh_r.at[5], up),
        remote(N.at[0:CT, NB, 8 + rows - M : 8 + rows, :], N.at[0:CT, NB, T2 + M : T2 + 2 * M, :], rh_s.at[6], rh_r.at[6], down),
    ]

    for cp in loads:
        cp.wait()
    for cp in swaps:
        cp.wait_recv()

    G = LANES // M
    groups = [(gi, min(G, NB + 1 - gi * G)) for gi in range(2)]
    for gi, cnt in groups:
        acc = [jnp.zeros((8, LANES), F32)] * 4
        for e in range(cnt):
            here = (lane >= e * M) & (lane < e * M + M)
            for h in range(2):
                a = N[0, gi * G + e, 8 + 8 * h : 16 + 8 * h, :]
                b = N[CT - 1, gi * G + e, 8 + 8 * h : 16 + 8 * h, :]
                acc[2 * h] = jnp.where(here, pltpu.roll(a, e * M, 1), acc[2 * h])
                acc[2 * h + 1] = jnp.where(here, pltpu.roll(b, (e * M + M) % LANES, 1), acc[2 * h + 1])
        for h in range(2):
            PL[gi, 8 * h : 8 * h + 8, :] = acc[2 * h]
            PR[gi, 8 * h : 8 * h + 8, :] = acc[2 * h + 1]

    strips = [
        remote(PL, RR.at[:, 0:rows, :], st_s.at[0], st_r.at[0], left),
        remote(PR, RL.at[:, 0:rows, :], st_s.at[1], st_r.at[1], right),
        remote(PL.at[:, 0:M, :], RR.at[:, rows : rows + M, :], st_s.at[2], st_r.at[2], corners[0]),
        remote(PR.at[:, 0:M, :], RL.at[:, rows : rows + M, :], st_s.at[3], st_r.at[3], corners[1]),
        remote(PL.at[:, rows - M : rows, :], RR.at[:, rows + M : rows + 2 * M, :], st_s.at[4], st_r.at[4], corners[2]),
        remote(PR.at[:, rows - M : rows, :], RL.at[:, rows + M : rows + 2 * M, :], st_s.at[5], st_r.at[5], corners[3]),
    ]
    for cp in strips:
        cp.start()
    for cp in (margins[0], margins[5], margins[6]):
        cp.start()

    def unpack(ks):
        for gi, cnt in groups:
            for k in ks:
                r = RR[gi, 8 * k : 8 * k + 8, :]
                l = RL[gi, 8 * k : 8 * k + 8, :]
                for e in range(cnt):
                    N[CT, gi * G + e, 8 + 8 * k : 16 + 8 * k, :] = jnp.where(
                        lane < LANES // 2,
                        pltpu.roll(r, (LANES - e * M) % LANES, 1),
                        pltpu.roll(l, (2 * LANES - M - e * M) % LANES, 1),
                    )

    first = lane == 0
    last = lane == LANES - 1

    def sl(r0, off=0):
        return slice(r0 + off, r0 + off + 8)

    def dual(it, r0):
        k = r0 // 8 - 1
        src = N if it == 0 else UB

        def body(b, acc):
            ub = [src[c, b, sl(r0), :] for c in range(C)]
            rolled = [pltpu.roll(v, LANES - 1, 1) for v in ub]
            out = []
            for c in range(C):
                below = src[c, b, sl(r0, 1), :]
                rightv = jnp.where(last, rolled[(c + 1) % C], rolled[c])
                qx = MX[k, c] * (below - ub[c])
                qy = MY[k, c] * (rightv - ub[c])
                if it > 0:
                    qx = qx + PX[c, b, sl(r0), :]
                    qy = qy + PY[c, b, sl(r0), :]
                QX[c, b, sl(r0), :] = qx
                QY[c, b, sl(r0), :] = qy
                if r0 == T2:
                    QX[c, b, 0:8, :] = qx
                elif it == 0 and r0 == O0:
                    N[c, b, 32:40, :] = ub[c]
                if r0 != T2:
                    out.append(acc[c] + (qx * qx + qy * qy))
            return tuple(out)

        init = () if r0 == T2 else (jnp.zeros((8, LANES), F32),) * C
        acc = lax.fori_loop(0, NB, body, init, unroll=UNROLL_B)
        if r0 != T2:
            for c in range(C):
                SB[it, k * C + c] = acc[c]

    def primal(it, r0):
        sc = [SC[it, c, sl(r0), :] for c in range(C)]
        scu = None if r0 == T2 else [SC[it, c, sl(r0, -1), :] for c in range(C)]

        def body(b, carry):
            py = [sc[c] * QY[c, b, sl(r0), :] for c in range(C)]
            rolled = [pltpu.roll(v, 1, 1) for v in py]
            px = [sc[c] * QX[c, b, sl(r0), :] for c in range(C)]
            for c in range(C):
                PX[c, b, sl(r0), :] = px[c]
            for c in range(C):
                if r0 == T2:
                    pxu = PX[c, b, sl(r0, -1), :]
                else:
                    pxu = scu[c] * QX[c, b, sl(r0, -1), :]
                pyl = jnp.where(first, rolled[(c - 1) % C], rolled[c])
                div = (px[c] - pxu) + (py[c] - pyl)
                n = N[c, b, sl(r0), :]
                if it == 0:
                    old = n
                    new = n + div
                else:
                    old = U[c, b, sl(r0), :]
                    new = C0 * old + (KAPPA * n + div)
                ubar = 2.0 * new - old
                PY[c, b, sl(r0), :] = py[c]
                U[c, b, sl(r0), :] = new
                UB[c, b, sl(r0), :] = ubar
                if r0 == O0:
                    UB[c, b, 32:40, :] = ubar
            return carry

        lax.fori_loop(0, NB, body, 0, unroll=UNROLL_A)

    def final(it, r0, own):
        sc = [SC[it, c, sl(r0), :] for c in range(C)]
        scu = [SC[it, c, sl(r0, -1), :] for c in range(CT)]
        base = (core if own else 1 - core) * bands

        def body(i, carry):
            b = base + i
            py = [sc[c] * QY[c, b, sl(r0), :] for c in range(C)]
            rolled = [pltpu.roll(v, 1, 1) for v in py]
            for c in range(CT):
                px = sc[c] * QX[c, b, sl(r0), :]
                pxu = scu[c] * QX[c, b, sl(r0, -1), :]
                pyl = jnp.where(first, rolled[(c - 1) % C], rolled[c])
                div = (px - pxu) + (py[c] - pyl)
                new = C0 * U[c, b, sl(r0), :] + (KAPPA * N[c, b, sl(r0), :] + div)
                if own:
                    out_ref[i, r0 - 8 : r0, lanes_of(core, c)] = new
                else:
                    OUT[c, i, r0 - 8 : r0, :] = new
            return carry

        lax.fori_loop(0, bands, body, 0, unroll=UNROLL_A)

    pending = list(swaps) + strips + below + margins

    def step(it, n, h):
        src, dst = ((SB, RB1), (TB, RB2))[n]
        a, b = h * C, h * C + C
        return remote(src.at[it, a:b], dst.at[it, a:b], ar_s.at[it, n, h], ar_r.at[it, n, h], (zA, zB)[(n + h) % 2])

    steps = [[[step(it, n, h) for h in range(2)] for n in range(2)] for it in range(ITERS)]

    def edge(it, h, n):
        if h == 0:
            src, dst, to = TB.at[it, 0:C, 0:M, :], ELO.at[it, n, :, 0:M, :], (up, up_zB)[n]
        else:
            src, dst, to = TB.at[it, C : 2 * C, 8 - M : 8, :], EUP.at[it, n, :, 8 - M : 8, :], (down, down_zA)[n]
        return remote(src, dst, e_s.at[it, h, n], e_r.at[it, h, n], to)

    edges = [[[edge(it, h, n) for n in range(2)] for h in range(2)] for it in range(ITERS)]

    def forward(it, h):
        steps[it][0][h].wait_recv()
        for t in range(h * C, h * C + C):
            TB[it, t] = SB[it, t] + RB1[it, t]
        steps[it][1][h].start()
        if h == 1 or it < ITERS - 1:
            for cp in edges[it][h]:
                cp.start()
                pending.append(cp)

    def scale_of(w, s):
        return w / jnp.maximum(w, jnp.sqrt(1.0 + s * (1.0 / (KAPPA * KAPPA))))

    def scales(it, h):
        steps[it][1][h].wait_recv()
        r0 = (O0, O1)[h]
        for c in range(C):
            t = h * C + c
            SC[it, c, sl(r0), :] = scale_of(N[c, NB, sl(r0), :], TB[it, t] + RB2[it, t])

    def scales_above(it):
        for cp in edges[it][1]:
            cp.wait_recv()
        for c in range(C):
            SC[it, c, 0:8, :] = scale_of(N[c, NB, sl(T2), :], EUP[it, 0, c] + EUP[it, 1, c])

    def scales_margin(it):
        for cp in edges[it][0]:
            cp.wait_recv()
        for c in range(C):
            lo = scale_of(N[c, NB, sl(T2), :], ELO[it, 0, c] + ELO[it, 1, c])
            SC[it, c, sl(T2), :] = jnp.where(sub < M, lo, SC[it, c, 0:8, :])

    for cp in strips[:2]:
        cp.wait_recv()
    unpack((0, 1))
    dual(0, O0)
    steps[0][0][0].start()
    for cp in strips[2:]:
        cp.wait_recv()
    unpack((2,))
    for t in range(2):
        for c in range(CT):
            below_arrival(t, c).wait_recv()
    dual(0, O1)
    steps[0][0][1].start()
    margins[1].start()
    margins[2].start()
    for it in range(ITERS):
        pending += steps[it][0] + steps[it][1]
        forward(it, 0)
        forward(it, 1)
        if it == 1:
            for cp in margins[3:5]:
                cp.wait_recv()
            mid = (sub >= 2) & (sub < 6)

            def merge(b, carry):
                for c in range(CT):
                    N[c, b, sl(T2), :] = jnp.where(mid, N2[c, b], N[c, b, sl(T2), :])
                return carry

            lax.fori_loop(0, NB, merge, 0, unroll=8)
            dual(0, T2)
            primal(0, T2)
            dual(1, T2)
        scales(it, 0)
        scales(it, 1)
        if it == ITERS - 1:
            final(it, O1, False)
            scales_above(it)
            final(it, O0, False)
            outs = [
                remote(OUT.at[c], out_ref.at[:, :, lanes_of(core, c)], o_s.at[c], o_r.at[c], partner)
                for c in range(CT)
            ]
            for cp in outs:
                cp.start()
            final(it, O1, True)
            final(it, O0, True)
            continue
        if it == 0:
            margins[3].start()
            margins[4].start()
        primal(it, O1)
        if it == 0:
            for cp in margins[0:3] + margins[5:7]:
                cp.wait_recv()
            dual(0, T2)
        scales_above(it)
        primal(it, O0)
        dual(it + 1, O0)
        steps[it + 1][0][0].start()
        scales_margin(it)
        primal(it, T2)
        dual(it + 1, O1)
        steps[it + 1][0][1].start()
        dual(it + 1, T2)

    for cp in pending:
        cp.wait_send()
    for cp in outs:
        cp.wait()


def solution(mesh):
    dims = tuple(mesh.shape[a] for a in ("row", "col", "band"))

    def local(noisy, weight_map):
        bands, rows, cols = noisy.shape
        NB = 2 * bands
        CT = cols // 2 // LANES
        C = CT + 1
        vm = lambda *s: pltpu.VMEM(s, F32)
        big = lambda: vm(C, NB + 1, SROWS, LANES)
        dma = lambda *s: pltpu.SemaphoreType.DMA(s)
        half_sums = lambda: vm(ITERS, 2 * C, 8, LANES)
        return pl.pallas_call(
            functools.partial(kernel, dims),
            out_shape=jax.ShapeDtypeStruct(noisy.shape, F32),
            in_specs=[pl.BlockSpec(memory_space=pl.ANY)] * 2,
            out_specs=pl.BlockSpec(memory_space=pltpu.VMEM),
            scratch_shapes=[
                big(), vm(CT, NB, 8, LANES), big(), big(), big(), big(), big(), big(),
                vm(ITERS, C, SROWS, LANES), vm(ITERS, 2, C, 8, LANES), vm(ITERS, 2, C, 8, LANES),
                vm(3, C, 8, LANES), vm(3, C, 8, LANES), vm(CT, bands, rows, LANES),
                vm(2, rows, LANES), vm(2, rows, LANES), vm(2, rows + 2 * M, LANES), vm(2, rows + 2 * M, LANES),
                half_sums(), half_sums(), half_sums(), half_sums(),
                dma(CT), dma(CT), dma(CT), dma(CT), dma(2, CT), dma(2, CT), dma(7), dma(7), dma(6), dma(6),
                dma(ITERS, 2, 2), dma(ITERS, 2, 2), dma(ITERS, 2, 2), dma(ITERS, 2, 2), dma(CT), dma(CT),
            ],
            compiler_params=pltpu.CompilerParams(
                collective_id=0, has_side_effects=True, vmem_limit_bytes=52 * 1024 * 1024
            ),
        )(noisy, weight_map)

    return jax.shard_map(
        local, mesh=mesh, in_specs=(P("band", "row", "col"), P("row", "col")),
        out_specs=P("band", "row", "col"), check_vma=False,
    )
```

time: 88.7 us -> 74.1 us (0.84)
  Pallas kernels: 85.7 us -> 71.8 us
    pallas_call x1, Pallas kernels: 85.7 us -> 71.8 us  [local(): pl.pallas_call(functools.partial(kernel, dims), out_shape=jax.ShapeDtypeS...]
    unnamed x1 -> x3, local copies, waits for them, and re-layouts: 2.94 us -> 2.07 us
where the time goes in v3:
time: 74.1 us; the launch traced here: 73.9 us
  Pallas kernels  71.8 us (97%)
  local copies, waits for them, and re-layouts  2.07 us (3%)
    pallas_call x1, Pallas kernels, local(): pl.pallas_call(functools.partial(kernel, dims), out_shape=jax.ShapeDtypeS...  71.8 us
    unnamed x3, local copies, waits for them, and re-layouts  2.07 us

profile of v3, /device:TPU:1, one launch (start us, length us, event | category | flops | bytes accessed | tf_op | source)
XLA Modules:
  0.0 73.9 jit_solution(15609715131779675473)
XLA Ops:
  0.0 0.0 copy-start
  0.0 0.8 %copy-done = f32[16,1024]{1,0:T(8,128)S(1)} copy-done((f32[16,1024]{1,0:T(8,128)S(1)}, f32[16,1024]{1,0:T(8,128)}, u32[]{:S(2)}) %copy-start) | copy-done | bytes 65560
  0.8 71.8 %shard_map.28 = f32[28,16,1024]{2,1,0:T(8,128)S(1)} custom-call(f32[28,16,1024]{2,1,0:T(8,128)} %noisy_ref.1, f32[16,1024]{1,0:T(8,128)S(1)} %copy-done), custom_call_target="tpu_custom_call" | custom-call | tf_op jit(solution)/shard_map/pallas_call | solution.py:402
  72.7 1.2 %copy.4 = f32[28,16,1024]{2,1,0:T(8,128)} copy(f32[28,16,1024]{2,1,0:T(8,128)S(1)} %shard_map.28) | data formatting | bytes 3670016
Async XLA Ops:
  0.0 0.8 %copy-start = (f32[16,1024]{1,0:T(8,128)S(1)}, f32[16,1024]{1,0:T(8,128)}, u32[]{:S(2)}) copy-start(f32[16,1024]{1,0:T(8,128)} %weight_ref.1) | copy-start | bytes 196612

commit v4 on v3

--- a/solution.py
+++ b/solution.py
@@ -23,8 +23,8 @@
 
 
 def kernel(dims, noisy_ref, weight_ref, out_ref, N, N2, U, UB, PX, PY, QX, QY, SC, ELO, EUP, MX, MY, OUT,
-           PL, PR, RL, RR, SB, RB1, TB, RB2,
-           s_in, s_w, sw_s, sw_r, g_s, g_r, rh_s, rh_r, st_s, st_r, ar_s, ar_r, e_s, e_r, o_s, o_r):
+           E, ST, R, SB, RB1, TB, RB2,
+           s_in, s_w, s_e, sw_s, sw_r, g_s, g_r, rh_s, rh_r, st_s, st_r, ar_s, ar_r, e_s, e_r, o_s, o_r):
     nrow, ncol, nband = dims
     bands, rows, cols = noisy_ref.shape
     NB = 2 * bands
@@ -36,7 +36,7 @@
     band = lax.axis_index("band")
     zc = nband // 2
     z = band // 2
-    core = band % 2
+    core = (band + z) % 2
     g = col * 2 + core
     ng = ncol * 2
 
@@ -44,11 +44,10 @@
         rr = (row + r + nrow) % nrow
         gg = g if gc is None else (gc + ng) % ng
         zz = z if zz is None else zz
-        return {"row": rr, "col": gg // 2, "band": zz * 2 + gg % 2}
-
-    partner = {"row": row, "col": col, "band": z * 2 + 1 - core}
-    up, down, left, right = dev(-1), dev(1), dev(0, g - 1), dev(0, g + 1)
-    corners = (dev(-1, g - 1), dev(-1, g + 1), dev(1, g - 1), dev(1, g + 1))
+        return {"row": rr, "col": gg // 2, "band": zz * 2 + (gg + zz) % 2}
+
+    partner = {"row": row, "col": col, "band": z * 2 + (1 - core + z) % 2}
+    up, down = dev(-1), dev(1)
     iA, iB = z + 1 - 2 * (z % 2), zc - 1 - z
     zA, zB = dev(zz=iA), dev(zz=iB)
     up_zB, down_zA, up_zA, down_zB = dev(-1, zz=iB), dev(1, zz=iA), dev(-1, zz=iA), dev(1, zz=iB)
@@ -58,7 +57,8 @@
         return pl.ds(pl.multiple_of(t * half + c * LANES, LANES), LANES)
 
     barrier = pltpu.get_barrier_semaphore()
-    peers = (up_zB, down_zA, up_zA, down_zB) + corners + (up, down, zA, zB, left, right)
+    beside = [(r, d) for d in (-2, -1, 1, 2) for r in (-1, 1, 0)]
+    peers = [up_zB, down_zA, up_zA, down_zB] + [dev(r, g + d) for r, d in beside] + [up, down, zA, zB]
     for d in peers:
         pl.semaphore_signal(barrier, inc=1, device_id=d, device_id_type=MESH)
 
@@ -66,6 +66,9 @@
     for c in range(CT):
         loads.append(pltpu.make_async_copy(noisy_ref.at[:, :, lanes_of(core, c)], N.at[c, mine, 8 : 8 + rows, :], s_in.at[c]))
         loads.append(pltpu.make_async_copy(weight_ref.at[:, lanes_of(core, c)], N.at[c, NB, 8 : 8 + rows, :], s_w.at[c]))
+    for i, at in enumerate(((CT - 1) * (1 - core), (CT - 1) * core)):
+        lanes = pl.ds(pl.multiple_of((1 - core) * half + at * LANES, LANES), LANES)
+        loads.append(pltpu.make_async_copy(noisy_ref.at[:, :, lanes], E.at[i], s_e.at[i]))
     for cp in loads:
         cp.start()
 
@@ -86,6 +89,24 @@
             MX[k, c] = jnp.where(kx, coef, 0.0).astype(F32)
             MY[k, c] = jnp.where(ky, coef, 0.0).astype(F32)
 
+    for cp in loads:
+        cp.wait()
+
+    for h in range(2):
+        tile_rows = slice(8 + 8 * h, 16 + 8 * h)
+        acc = [jnp.zeros((8, LANES), F32)] * 4
+        for e in range(bands + 1):
+            here = (lane >= e * M) & (lane < e * M + M)
+            own = core * bands + e if e < bands else NB
+            acc[0] = jnp.where(here, pltpu.roll(N[0, own, tile_rows, :], e * M, 1), acc[0])
+            acc[1] = jnp.where(here, pltpu.roll(N[CT - 1, own, tile_rows, :], (e * M + M) % LANES, 1), acc[1])
+            if e < bands:
+                acc[2] = jnp.where(here, pltpu.roll(E[0, e, 8 * h : 8 * h + 8, :], e * M + M * (1 - core), 1), acc[2])
+                acc[3] = jnp.where(here, pltpu.roll(E[1, e, 8 * h : 8 * h + 8, :], e * M + M * core, 1), acc[3])
+        for i in range(4):
+            ST[i, 8 * h : 8 * h + 8, :] = acc[i]
+        R[core, core, 8 * h : 8 * h + 8, :] = acc[3]
+
     pl.semaphore_wait(barrier, len(peers))
 
     def remote(src, dst, ss, rs, d):
@@ -99,75 +120,71 @@
     for cp in swaps:
         cp.start()
 
-    def below_piece(t, c):
-        return remote(noisy_ref.at[:, 0:1, lanes_of(t, c)], N.at[c, mine, T2 : T2 + 1, :],
-                      g_s.at[t, c], g_r.at[core, c], dev(-1, col * 2 + t))
-
-    def below_arrival(t, c):
-        at = N.at[c, pl.ds(t * bands, bands), T2 : T2 + 1, :]
-        return remote(at, at, g_s.at[t, c], g_r.at[t, c], partner)
-
-    below = [below_piece(t, c) for c in range(CT) for t in range(2)]
-    for cp in below:
+    strips = []
+    for i, (side, shift) in enumerate(((0, -1), (1, 1), (1 - core, 2 - 4 * core), (core, 0))):
+        for part, (r, src, dst) in enumerate(((0, 0, 0), (-1, 0, rows), (1, rows - M, rows + M))):
+            if i == 3 and part == 0:
+                continue
+            n = rows if part == 0 else M
+            strips.append(remote(ST.at[i, src : src + n, :], R.at[side, core, dst : dst + n, :],
+                                 st_s.at[i, part], st_r.at[side, core, part], dev(r, g + shift)))
+    for cp in strips:
         cp.start()
 
-    def margin(i, src0, dst, to):
-        return remote(N.at[0:CT, 0:NB, 8 + src0[0] : 8 + src0[1], :], dst, rh_s.at[i], rh_r.at[i], to)
+    def strip_arrival(side, src, part):
+        n = rows if part == 0 else M
+        at = R.at[side, src, (0, rows, rows + M)[part] : (0, rows, rows + M)[part] + n, :]
+        return remote(at, at, st_s.at[0, 0], st_r.at[side, src, part], partner)
+
+    def next_row(d, t, c):
+        src0, dst0 = (0, 0) if d == 0 else (rows - 1, 2 * M - 1)
+        return remote(noisy_ref.at[:, src0 : src0 + 1, lanes_of(t, c)], N.at[c, mine, T2 + dst0 : T2 + dst0 + 1, :],
+                      g_s.at[d, t, c], g_r.at[d, core, c], dev(-1 if d == 0 else 1, col * 2 + t))
+
+    def next_row_arrival(d, t, c):
+        at = N.at[c, pl.ds(t * bands, bands), T2 + (2 * M - 1) * d : T2 + (2 * M - 1) * d + 1, :]
+        return remote(at, at, g_s.at[d, t, c], g_r.at[d, t, c], partner)
+
+    nexts = [next_row(d, t, c) for d in range(2) for c in range(CT) for t in range(2)]
+    for cp in nexts:
+        cp.start()
+
+    def margin(i, src0, dst, dst0, to):
+        return remote(N.at[0:CT, 0:NB, 8 + src0 : 9 + src0, :], dst.at[0:CT, 0:NB, dst0 : dst0 + 1, :], rh_s.at[i], rh_r.at[i], to)
 
     margins = [
-        margin(0, (rows - 1, rows), N.at[0:CT, 0:NB, T2 + 7 : T2 + 8, :], down),
-        margin(1, (1, 2), N.at[0:CT, 0:NB, T2 + 1 : T2 + 2, :], up),
-        margin(2, (rows - 2, rows - 1), N.at[0:CT, 0:NB, T2 + 6 : T2 + 7, :], down),
-        margin(3, (2, 4), N2.at[:, :, 2:4, :], up),
-        margin(4, (rows - 4, rows - 2), N2.at[:, :, 4:6, :], down),
-        remote(N.at[0:CT, NB, 8 : 8 + M, :], N.at[0:CT, NB, T2 : T2 + M, :], rh_s.at[5], rh_r.at[5], up),
-        remote(N.at[0:CT, NB, 8 + rows - M : 8 + rows, :], N.at[0:CT, NB, T2 + M : T2 + 2 * M, :], rh_s.at[6], rh_r.at[6], down),
+        margin(0, 1, N, T2 + 1, up),
+        margin(1, rows - 2, N, T2 + 6, down),
+        margin(2, 2, N2, 2, up),
+        margin(3, rows - 3, N2, 5, down),
+        margin(4, 3, N2, 3, up),
+        margin(5, rows - 4, N2, 4, down),
+        remote(N.at[0:CT, NB, 8 : 8 + M, :], N.at[0:CT, NB, T2 : T2 + M, :], rh_s.at[6], rh_r.at[6], up),
+        remote(N.at[0:CT, NB, 8 + rows - M : 8 + rows, :], N.at[0:CT, NB, T2 + M : T2 + 2 * M, :], rh_s.at[7], rh_r.at[7], down),
     ]
 
-    for cp in loads:
-        cp.wait()
+    for cp in (margins[6], margins[7]):
+        cp.start()
     for cp in swaps:
         cp.wait_recv()
-
-    G = LANES // M
-    groups = [(gi, min(G, NB + 1 - gi * G)) for gi in range(2)]
-    for gi, cnt in groups:
-        acc = [jnp.zeros((8, LANES), F32)] * 4
-        for e in range(cnt):
-            here = (lane >= e * M) & (lane < e * M + M)
-            for h in range(2):
-                a = N[0, gi * G + e, 8 + 8 * h : 16 + 8 * h, :]
-                b = N[CT - 1, gi * G + e, 8 + 8 * h : 16 + 8 * h, :]
-                acc[2 * h] = jnp.where(here, pltpu.roll(a, e * M, 1), acc[2 * h])
-                acc[2 * h + 1] = jnp.where(here, pltpu.roll(b, (e * M + M) % LANES, 1), acc[2 * h + 1])
-        for h in range(2):
-            PL[gi, 8 * h : 8 * h + 8, :] = acc[2 * h]
-            PR[gi, 8 * h : 8 * h + 8, :] = acc[2 * h + 1]
-
-    strips = [
-        remote(PL, RR.at[:, 0:rows, :], st_s.at[0], st_r.at[0], left),
-        remote(PR, RL.at[:, 0:rows, :], st_s.at[1], st_r.at[1], right),
-        remote(PL.at[:, 0:M, :], RR.at[:, rows : rows + M, :], st_s.at[2], st_r.at[2], corners[0]),
-        remote(PR.at[:, 0:M, :], RL.at[:, rows : rows + M, :], st_s.at[3], st_r.at[3], corners[1]),
-        remote(PL.at[:, rows - M : rows, :], RR.at[:, rows + M : rows + 2 * M, :], st_s.at[4], st_r.at[4], corners[2]),
-        remote(PR.at[:, rows - M : rows, :], RL.at[:, rows + M : rows + 2 * M, :], st_s.at[5], st_r.at[5], corners[3]),
-    ]
-    for cp in strips:
-        cp.start()
-    for cp in (margins[0], margins[5], margins[6]):
-        cp.start()
+    margins[0].start()
 
     def unpack(ks):
-        for gi, cnt in groups:
-            for k in ks:
-                r = RR[gi, 8 * k : 8 * k + 8, :]
-                l = RL[gi, 8 * k : 8 * k + 8, :]
-                for e in range(cnt):
-                    N[CT, gi * G + e, 8 + 8 * k : 16 + 8 * k, :] = jnp.where(
+        for k in ks:
+            for src in range(2):
+                right = R[0, src, 8 * k : 8 * k + 8, :]
+                left = R[1, src, 8 * k : 8 * k + 8, :]
+                for e in range(bands):
+                    N[CT, src * bands + e, 8 + 8 * k : 16 + 8 * k, :] = jnp.where(
                         lane < LANES // 2,
-                        pltpu.roll(r, (LANES - e * M) % LANES, 1),
-                        pltpu.roll(l, (2 * LANES - M - e * M) % LANES, 1),
+                        pltpu.roll(right, (LANES - e * M) % LANES, 1),
+                        pltpu.roll(left, (2 * LANES - M - e * M) % LANES, 1),
                     )
+            N[CT, NB, 8 + 8 * k : 16 + 8 * k, :] = jnp.where(
+                lane < LANES // 2,
+                pltpu.roll(R[0, 1 - core, 8 * k : 8 * k + 8, :], LANES - bands * M, 1),
+                pltpu.roll(R[1, 1 - core, 8 * k : 8 * k + 8, :], LANES - M - bands * M, 1),
+            )
 
     first = lane == 0
     last = lane == LANES - 1
@@ -264,7 +281,7 @@
 
         lax.fori_loop(0, bands, body, 0, unroll=UNROLL_A)
 
-    pending = list(swaps) + strips + below + margins
+    pending = list(swaps) + strips + nexts + margins
 
     def step(it, n, h):
         src, dst = ((SB, RB1), (TB, RB2))[n]
@@ -315,27 +332,32 @@
             lo = scale_of(N[c, NB, sl(T2), :], ELO[it, 0, c] + ELO[it, 1, c])
             SC[it, c, sl(T2), :] = jnp.where(sub < M, lo, SC[it, c, 0:8, :])
 
-    for cp in strips[:2]:
-        cp.wait_recv()
+    for side, src in ((core, 1 - core), (1 - core, 0), (1 - core, 1)):
+        strip_arrival(side, src, 0).wait_recv()
     unpack((0, 1))
     dual(0, O0)
     steps[0][0][0].start()
-    for cp in strips[2:]:
-        cp.wait_recv()
+    for side in range(2):
+        for src in range(2):
+            for part in (1, 2):
+                strip_arrival(side, src, part).wait_recv()
     unpack((2,))
     for t in range(2):
         for c in range(CT):
-            below_arrival(t, c).wait_recv()
+            next_row_arrival(0, t, c).wait_recv()
     dual(0, O1)
     steps[0][0][1].start()
     margins[1].start()
-    margins[2].start()
     for it in range(ITERS):
         pending += steps[it][0] + steps[it][1]
-        forward(it, 0)
-        forward(it, 1)
+        order = (0, 1) if it == 0 else (1, 0)
+        for h in order:
+            forward(it, h)
+        if it == 0:
+            for cp in margins[2:5]:
+                cp.start()
         if it == 1:
-            for cp in margins[3:5]:
+            for cp in margins[2:6]:
                 cp.wait_recv()
             mid = (sub >= 2) & (sub < 6)
 
@@ -348,37 +370,41 @@
             dual(0, T2)
             primal(0, T2)
             dual(1, T2)
-        scales(it, 0)
-        scales(it, 1)
+        for h in order:
+            scales(it, h)
         if it == ITERS - 1:
             final(it, O1, False)
+            outs = [
+                remote(OUT.at[c, :, 8 * h : 8 * h + 8, :], out_ref.at[:, 8 * h : 8 * h + 8, lanes_of(core, c)], o_s.at[h, c], o_r.at[h, c], partner)
+                for h in (1, 0) for c in range(CT)
+            ]
+            for cp in outs[:CT]:
+                cp.start()
             scales_above(it)
             final(it, O0, False)
-            outs = [
-                remote(OUT.at[c], out_ref.at[:, :, lanes_of(core, c)], o_s.at[c], o_r.at[c], partner)
-                for c in range(CT)
-            ]
-            for cp in outs:
+            for cp in outs[CT:]:
                 cp.start()
             final(it, O1, True)
             final(it, O0, True)
             continue
-        if it == 0:
-            margins[3].start()
-            margins[4].start()
         primal(it, O1)
         if it == 0:
-            for cp in margins[0:3] + margins[5:7]:
+            for t in range(2):
+                for c in range(CT):
+                    next_row_arrival(1, t, c).wait_recv()
+            for cp in margins[0:2] + margins[6:8]:
                 cp.wait_recv()
             dual(0, T2)
         scales_above(it)
         primal(it, O0)
-        dual(it + 1, O0)
-        steps[it + 1][0][0].start()
         scales_margin(it)
         primal(it, T2)
         dual(it + 1, O1)
         steps[it + 1][0][1].start()
+        dual(it + 1, O0)
+        steps[it + 1][0][0].start()
+        if it == 0:
+            margins[5].start()
         dual(it + 1, T2)
 
     for cp in pending:
@@ -408,10 +434,10 @@
                 big(), vm(CT, NB, 8, LANES), big(), big(), big(), big(), big(), big(),
                 vm(ITERS, C, SROWS, LANES), vm(ITERS, 2, C, 8, LANES), vm(ITERS, 2, C, 8, LANES),
                 vm(3, C, 8, LANES), vm(3, C, 8, LANES), vm(CT, bands, rows, LANES),
-                vm(2, rows, LANES), vm(2, rows, LANES), vm(2, rows + 2 * M, LANES), vm(2, rows + 2 * M, LANES),
+                vm(2, bands, rows, LANES), vm(4, rows, LANES), vm(2, 2, rows + 2 * M, LANES),
                 half_sums(), half_sums(), half_sums(), half_sums(),
-                dma(CT), dma(CT), dma(CT), dma(CT), dma(2, CT), dma(2, CT), dma(7), dma(7), dma(6), dma(6),
-                dma(ITERS, 2, 2), dma(ITERS, 2, 2), dma(ITERS, 2, 2), dma(ITERS, 2, 2), dma(CT), dma(CT),
+                dma(CT), dma(CT), dma(2), dma(CT), dma(CT), dma(2, 2, CT), dma(2, 2, CT), dma(8), dma(8), dma(4, 3), dma(2, 2, 3),
+                dma(ITERS, 2, 2), dma(ITERS, 2, 2), dma(ITERS, 2, 2), dma(ITERS, 2, 2), dma(2, CT), dma(2, CT),
             ],
             compiler_params=pltpu.CompilerParams(
                 collective_id=0, has_side_effects=True, vmem_limit_bytes=52 * 1024 * 1024

time: 74.1 us -> 68.1 us (0.919)
  Pallas kernels: 71.8 us -> 65.9 us
    pallas_call x1, Pallas kernels: 71.8 us -> 65.9 us  [local(): pl.pallas_call(functools.partial(kernel, dims), out_shape=jax.ShapeDtypeS...]
where the time goes in v4:
time: 68.1 us; the launch traced here: 68 us
  Pallas kernels  65.9 us (97%)
  local copies, waits for them, and re-layouts  2.07 us (3%)
    pallas_call x1, Pallas kernels, local(): pl.pallas_call(functools.partial(kernel, dims), out_shape=jax.ShapeDtypeS...  65.9 us
    unnamed x3, local copies, waits for them, and re-layouts  2.07 us

profile of v4, /device:TPU:1, one launch (start us, length us, event | category | flops | bytes accessed | tf_op | source)
XLA Modules:
  0.0 68.0 jit_solution(1146820489796968013)
XLA Ops:
  0.0 0.0 copy-start
  0.0 0.8 %copy-done = f32[16,1024]{1,0:T(8,128)S(1)} copy-done((f32[16,1024]{1,0:T(8,128)S(1)}, f32[16,1024]{1,0:T(8,128)}, u32[]{:S(2)}) %copy-start) | copy-done | bytes 65560
  0.8 65.9 %shard_map.28 = f32[28,16,1024]{2,1,0:T(8,128)S(1)} custom-call(f32[28,16,1024]{2,1,0:T(8,128)} %noisy_ref.1, f32[16,1024]{1,0:T(8,128)S(1)} %copy-done), custom_call_target="tpu_custom_call" | custom-call | tf_op jit(solution)/shard_map/pallas_call | solution.py:428
  66.8 1.2 %copy.4 = f32[28,16,1024]{2,1,0:T(8,128)} copy(f32[28,16,1024]{2,1,0:T(8,128)S(1)} %shard_map.28) | data formatting | bytes 3670016
Async XLA Ops:
  0.0 0.8 %copy-start = (f32[16,1024]{1,0:T(8,128)S(1)}, f32[16,1024]{1,0:T(8,128)}, u32[]{:S(2)}) copy-start(f32[16,1024]{1,0:T(8,128)} %weight_ref.1) | copy-start | bytes 196612

commit v5 on v4

--- a/solution.py
+++ b/solution.py
@@ -18,11 +18,11 @@
 F32 = jnp.float32
 O0, O1, T2 = 8, 16, 24
 SROWS = 40
-UNROLL_B = 14
+UNROLL_B = 28
 UNROLL_A = 14
 
 
-def kernel(dims, noisy_ref, weight_ref, out_ref, N, N2, U, UB, PX, PY, QX, QY, SC, ELO, EUP, MX, MY, OUT,
+def kernel(dims, noisy_ref, weight_ref, out_ref, N, N2, U, UB, PX, QX, QY, SC, ELO, EUP, MX, MY, OUT,
            E, ST, R, SB, RB1, TB, RB2,
            s_in, s_w, s_e, sw_s, sw_r, g_s, g_r, rh_s, rh_r, st_s, st_r, ar_s, ar_r, e_s, e_r, o_s, o_r):
     nrow, ncol, nband = dims
@@ -206,8 +206,9 @@
                 qx = MX[k, c] * (below - ub[c])
                 qy = MY[k, c] * (rightv - ub[c])
                 if it > 0:
-                    qx = qx + PX[c, b, sl(r0), :]
-                    qy = qy + PY[c, b, sl(r0), :]
+                    sc = SC[it - 1, c, sl(r0), :]
+                    qx = qx + sc * QX[c, b, sl(r0), :]
+                    qy = qy + sc * QY[c, b, sl(r0), :]
                 QX[c, b, sl(r0), :] = qx
                 QY[c, b, sl(r0), :] = qy
                 if r0 == T2:
@@ -226,16 +227,19 @@
 
     def primal(it, r0):
         sc = [SC[it, c, sl(r0), :] for c in range(C)]
-        scu = None if r0 == T2 else [SC[it, c, sl(r0, -1), :] for c in range(C)]
+        keep = it == 0 and r0 != O0
+        through = it == 0 and r0 == T2
+        scu = None if through else [SC[it, c, sl(r0, -1), :] for c in range(C)]
 
         def body(b, carry):
             py = [sc[c] * QY[c, b, sl(r0), :] for c in range(C)]
             rolled = [pltpu.roll(v, 1, 1) for v in py]
             px = [sc[c] * QX[c, b, sl(r0), :] for c in range(C)]
+            if keep:
+                for c in range(C):
+                    PX[c, b, sl(r0), :] = px[c]
             for c in range(C):
-                PX[c, b, sl(r0), :] = px[c]
-            for c in range(C):
-                if r0 == T2:
+                if through:
                     pxu = PX[c, b, sl(r0, -1), :]
                 else:
                     pxu = scu[c] * QX[c, b, sl(r0, -1), :]
@@ -249,7 +253,6 @@
                     old = U[c, b, sl(r0), :]
                     new = C0 * old + (KAPPA * n + div)
                 ubar = 2.0 * new - old
-                PY[c, b, sl(r0), :] = py[c]
                 U[c, b, sl(r0), :] = new
                 UB[c, b, sl(r0), :] = ubar
                 if r0 == O0:
@@ -431,7 +434,7 @@
             in_specs=[pl.BlockSpec(memory_space=pl.ANY)] * 2,
             out_specs=pl.BlockSpec(memory_space=pltpu.VMEM),
             scratch_shapes=[
-                big(), vm(CT, NB, 8, LANES), big(), big(), big(), big(), big(), big(),
+                big(), vm(CT, NB, 8, LANES), big(), big(), big(), big(), big(),
                 vm(ITERS, C, SROWS, LANES), vm(ITERS, 2, C, 8, LANES), vm(ITERS, 2, C, 8, LANES),
                 vm(3, C, 8, LANES), vm(3, C, 8, LANES), vm(CT, bands, rows, LANES),
                 vm(2, bands, rows, LANES), vm(4, rows, LANES), vm(2, 2, rows + 2 * M, LANES),

time: 68.1 us -> 67.9 us (level)
  no operation moved by 1% of the time
where the time goes in v5:
time: 67.9 us; the launch traced here: 67.8 us
  Pallas kernels  65.7 us (97%)
  local copies, waits for them, and re-layouts  2.07 us (3%)
    pallas_call x1, Pallas kernels, local(): pl.pallas_call(functools.partial(kernel, dims), out_shape=jax.ShapeDtypeS...  65.7 us
    unnamed x3, local copies, waits for them, and re-layouts  2.07 us

profile of v5, /device:TPU:1, one launch (start us, length us, event | category | flops | bytes accessed | tf_op | source)
XLA Modules:
  0.0 67.8 jit_solution(17497755249753567793)
XLA Ops:
  0.0 0.0 copy-start
  0.0 0.8 %copy-done = f32[16,1024]{1,0:T(8,128)S(1)} copy-done((f32[16,1024]{1,0:T(8,128)S(1)}, f32[16,1024]{1,0:T(8,128)}, u32[]{:S(2)}) %copy-start) | copy-done | bytes 65560
  0.8 65.7 %shard_map.28 = f32[28,16,1024]{2,1,0:T(8,128)S(1)} custom-call(f32[28,16,1024]{2,1,0:T(8,128)} %noisy_ref.1, f32[16,1024]{1,0:T(8,128)S(1)} %copy-done), custom_call_target="tpu_custom_call" | custom-call | tf_op jit(solution)/shard_map/pallas_call | solution.py:431
  66.6 1.2 %copy.4 = f32[28,16,1024]{2,1,0:T(8,128)} copy(f32[28,16,1024]{2,1,0:T(8,128)S(1)} %shard_map.28) | data formatting | bytes 3670016
Async XLA Ops:
  0.0 0.8 %copy-start = (f32[16,1024]{1,0:T(8,128)S(1)}, f32[16,1024]{1,0:T(8,128)}, u32[]{:S(2)}) copy-start(f32[16,1024]{1,0:T(8,128)} %weight_ref.1) | copy-start | bytes 196612
